TPU v7x, 256 devices: a whole 4x4x8 slice. The times are simulated.
256 devices in a mesh: fsdp: 32 (over z, y), rep: 8 (over x, core).
Axes of the slice: x: 4, y: 4, z: 8, core: 2. Of those that a mesh axis runs over, the one named last changes fastest.
Arguments:
- hidden: bfloat16 [65536, 2048], P(('fsdp', 'rep')), may hold values from -6 to 6
- attn_gain: bfloat16 [2048], P(('fsdp', 'rep')), may hold values from 0.25 to 1.75
- w_query: bfloat16 [2048, 2048], P(('fsdp', 'rep')), as said below
- w_key: bfloat16 [2048, 512], P(('fsdp', 'rep')), as said below
- w_value: bfloat16 [2048, 512], P(('fsdp', 'rep')), may hold values from -0.125 to 0.125
- w_out: bfloat16 [2048, 2048], P(None, ('fsdp', 'rep')), may hold values from -0.125 to 0.125
Outputs:
- mixed: bfloat16 [65536, 2048], P(('fsdp', 'rep'))
Inputs may be any that keep to these rules, and one draw needn't show every extreme that they name: `w_query`: entries of order 2048^(-1/2). `w_key`: entries of order 2048^(-1/2) times a factor up to twenty.
All inputs are finite; a program needn't handle non-finite values.
Results may differ from a plain program's by a relative error of at most 0.012.
The roundings to bfloat16 on the way count: a program that leaves them out, or rounds other values in their place, can miss the bound.
Values may be sent and summed in bfloat16 or wider, within the bound.
A program may use at most 64 MiB of HBM per device.

v0:
```python
import jax
import jax.numpy as jnp
from jax import lax
from jax.sharding import PartitionSpec as P

HD = 64
rope_base = 500000.0
norm_eps = 1e-05


def sent_together(arrays, axis, dim, along):
    columns = [a.reshape(*a.shape[:along], -1) for a in arrays]
    both = jnp.concatenate(columns, axis=along)
    filled, at, gathered = (lax.all_gather(both, axis, axis=dim, tiled=True), 0, [])
    for a, column in zip(arrays, columns):
        piece = filled[..., at : at + column.shape[along]]
        gathered.append(piece.reshape(*piece.shape[:along], *a.shape[along:]))
        at += column.shape[along]
    return tuple(gathered)


def copy_for_each(array, axis):
    copies = jnp.broadcast_to(array, (lax.axis_size(axis), *array.shape))
    return lax.all_to_all(copies, axis, split_axis=0, concat_axis=0, tiled=True)


def laid_out(blocks, dim):
    blocks = jnp.moveaxis(blocks, 0, dim)
    dims = blocks.shape
    return blocks.reshape(*dims[:dim], dims[dim] * dims[dim + 1], *dims[dim + 2 :])


def gather_directly(array, axis, dim):
    blocks = copy_for_each(array, axis)
    return laid_out(blocks, dim)


def rope_tables(tokens, head_dim):
    position = jnp.arange(tokens, dtype=jnp.float32)
    freq = rope_base ** (-(jnp.arange(head_dim // 2, dtype=jnp.float32) * 2.0) / head_dim)
    angle = position[:, None] * freq[None, :]
    cos_table = jnp.concatenate([jnp.cos(angle), jnp.cos(angle)], axis=-1)
    sin_table = jnp.concatenate([jnp.sin(angle), jnp.sin(angle)], axis=-1)
    return (cos_table, sin_table)


def rotate(tensor, cos_table, sin_table):
    half = tensor.shape[-1] // 2
    turned = jnp.concatenate([-tensor[..., half:], tensor[..., :half]], axis=-1)
    return tensor * cos_table + turned * sin_table


def body(hidden, attn_gain, w_query, w_key, w_value, w_out):
    tokens = hidden.shape[0]
    head_dim = HD
    width_query = w_query.shape[1]
    width_kv = w_key.shape[1]
    kv_count = width_kv // head_dim
    group = width_query // width_kv
    x_float = hidden.astype(jnp.float32)
    inv_rms = lax.rsqrt(jnp.mean(x_float * x_float, axis=-1, keepdims=True) + norm_eps)
    grouped = sent_together((attn_gain, w_query, w_key, w_value), "rep", 0, 1)
    gain_piece, query_piece, key_piece, value_piece = sent_together(
        (grouped[0], grouped[1], grouped[2], grouped[3]), "fsdp", 0, 1
    )
    normed = (x_float * inv_rms * gain_piece.astype(jnp.float32)[None, :]).astype(jnp.bfloat16)
    queries = jnp.dot(normed, query_piece, preferred_element_type=jnp.float32)
    keys_raw = jnp.dot(normed, key_piece, preferred_element_type=jnp.float32)
    values_raw = jnp.dot(normed, value_piece, preferred_element_type=jnp.float32)
    cos_table, sin_table = rope_tables(tokens, head_dim)
    queries = queries.reshape(tokens, kv_count, group, head_dim)
    keys_raw = keys_raw.reshape(tokens, kv_count, head_dim)
    values_bf = values_raw.reshape(tokens, kv_count, head_dim).astype(jnp.bfloat16)
    rope_queries = rotate(queries, cos_table[:, None, None, :], sin_table[:, None, None, :]).astype(
        jnp.bfloat16
    )
    rope_keys = rotate(keys_raw, cos_table[:, None, :], sin_table[:, None, :]).astype(jnp.bfloat16)
    scores = jnp.einsum(
        "qkgd,skd->kgqs", rope_queries, rope_keys, preferred_element_type=jnp.float32
    ) * head_dim ** (-0.5)
    causal = jnp.arange(tokens)[:, None] >= jnp.arange(tokens)[None, :]
    scores = jnp.where(causal[None, None, :, :], scores, -1e30)
    top = jnp.max(scores, axis=-1, keepdims=True)
    expo = jnp.exp(scores - top)
    probs = (expo / jnp.sum(expo, axis=-1, keepdims=True)).astype(jnp.bfloat16)
    context = jnp.einsum("kgqs,skd->qkgd", probs, values_bf, preferred_element_type=jnp.float32)
    context = context.reshape(tokens, width_query).astype(jnp.bfloat16)
    grouped_cols = gather_directly(w_out, "rep", 1)
    branch = jnp.dot(
        context,
        lax.all_gather(grouped_cols, "fsdp", axis=1, tiled=True),
        preferred_element_type=jnp.float32,
    )
    return (x_float + branch).astype(jnp.bfloat16)


def solution(mesh):
    placed = (
        P(("fsdp", "rep"), None),
        P(("fsdp", "rep")),
        P(("fsdp", "rep"), None),
        P(("fsdp", "rep"), None),
        P(("fsdp", "rep"), None),
        P(None, ("fsdp", "rep")),
    )
    return jax.shard_map(
        body, mesh=mesh, in_specs=placed, out_specs=P(("fsdp", "rep"), None), check_vma=False
    )
```

profile of v0, /device:TPU:1, one launch (start us, length us, event | category | flops | bytes accessed | tf_op | source)
XLA Modules:
  0.0 258.1 jit_solution(10988606192208036558)
XLA Ops:
  6.5 0.0 copy-start
  6.5 0.0 all-gather.3.cloned.1.call-start
  6.5 0.8 copy.17
  7.4 0.9 concatenate.17
  8.2 17.1 %all_gather.9 = bf16[64,3073]{1,0:T(8,128)(2,1)} all-gather(bf16[8,3073]{1,0:T(8,128)(2,1)S(1)} %concatenate.17), channel_id=1, replica_groups=mesh['fsdp'=32,'rep'=8] {'rep'}, dimensions={0}, use_global_device_ids=true | all-gather | bytes 442512 | tf_op jit(solution)/shard_map/all_gather | solution.py:14
  25.4 0.0 all-gather.3.cloned.1.call-update
  25.4 0.0 all-gather.5.cloned.1.call-start
  25.4 0.8 broadcast_in_dim.12
  26.2 9.7 %all_to_all.5 = bf16[8,2048,8]{1,2,0:T(8,128)(2,1)} all-to-all(bf16[8,2048,8]{1,2,0:T(8,128)(2,1)S(1)} %broadcast_in_dim.12), channel_id=1, replica_groups=mesh['fsdp'=32,'rep'=8] {'rep'}, dimensions={0} | all-to-all | bytes 524288 | tf_op jit(solution)/shard_map/all_to_all | solution.py:24
  35.9 0.0 all-gather.5.cloned.1.call-update
  36.0 0.2 fusion.33
  36.2 0.0 copy-done
  36.2 0.3 fusion.9
  36.5 110.4 %all-gather.3.cloned.1.call-done = bf16[2048,3073]{1,0:T(8,128)(2,1)} async-done(((bf16[64,3073]{1,0:T(8,128)(2,1)}), bf16[2048,3073]{1,0:T(8,128)(2,1)}) %all-gather.3.cloned.1.call-update) | async-done | bytes 12587024 | tf_op jit(solution)/shard_map/all_gather | solution.py:14
  146.9 1.3 convert_reduce_fusion
  148.2 2.9 %fusion.19 = bf16[256,512]{1,0:T(8,128)(2,1)S(1)} fusion(bf16[2048,3073]{1,0:T(8,128)(2,1)} %all-gather.3.cloned.1.call-done, bf16[256,2048]{1,0:T(8,128)(2,1)S(1)} %copy-done, f32[2048]{0:T(1024)S(1)} %convert_reduce_fusion, f32[256]{0:T(256)S(1)} %add_rsqrt_fusion), kind=kOutput, calls=%fused_computation.26 | convolution fusion | flops 539099136 | bytes 3417088 | tf_op jit(solution)/shard_map/dot_general | solution.py:69
  151.0 0.1 copy.18
  151.2 3.7 %fusion.12 = f32[256,512]{0,1:T(8,128)S(1)} fusion(bf16[2048,3073]{1,0:T(8,128)(2,1)} %all-gather.3.cloned.1.call-done, bf16[256,2048]{1,0:T(8,128)(2,1)S(1)} %copy-done, f32[2048]{0:T(1024)S(1)} %convert_reduce_fusion, f32[256]{0:T(256)S(1)} %add_rsqrt_fusion), kind=kOutput, calls=%fused_computation.18 | convolution fusion | flops 538968064 | bytes 3679232 | tf_op jit(solution)/shard_map/dot_general | solution.py:68
  154.9 10.6 %fusion.1 = f32[256,2048]{0,1:T(8,128)S(1)} fusion(bf16[2048,3073]{1,0:T(8,128)(2,1)} %all-gather.3.cloned.1.call-done, bf16[256,2048]{1,0:T(8,128)(2,1)S(1)} %copy-done, f32[2048]{0:T(1024)S(1)} %convert_reduce_fusion, f32[256]{0:T(256)S(1)} %add_rsqrt_fusion), kind=kOutput, calls=%fused_computation.1 | convolution fusion | flops 2149580800 | bytes 11543552 | tf_op jit(solution)/shard_map/dot_general | solution.py:67
  165.5 0.2 slice_negate_fusion
  165.7 1.5 fusion.22
  167.2 2.3 fusion.40
  169.5 0.9 fusion.18
  170.4 74.1 %all-gather.5.cloned.1.call-done = bf16[2048,2048]{0,1:T(8,128)(2,1)} async-done(((bf16[2048,64]{0,1:T(8,128)(2,1)}), bf16[2048,2048]{0,1:T(8,128)(2,1)}) %all-gather.5.cloned.1.call-update) | async-done | bytes 8388624 | tf_op jit(solution)/shard_map/all_gather | solution.py:91
  244.5 6.7 %fusion.8 = bf16[256,2048]{1,0:T(8,128)(2,1)} fusion(bf16[256,2048]{0,1:T(8,128)(2,1)S(1)} %bitcast.40, bf16[2048,2048]{0,1:T(8,128)(2,1)} %all-gather.5.cloned.1.call-done, bf16[256,2048]{1,0:T(8,128)(2,1)S(1)} %copy-done), kind=kOutput, calls=%fused_computation.14 | convolution fusion | flops 2149056512 | bytes 11534336 | tf_op jit(solution)/shard_map/dot_general | solution.py:89
  (5 shorter events, 0.1 us)
Async XLA Ops:
  6.5 29.7 %copy-start = (bf16[256,2048]{1,0:T(8,128)(2,1)S(1)}, bf16[256,2048]{1,0:T(8,128)(2,1)}, u32[]{:S(2)}) copy-start(bf16[256,2048]{1,0:T(8,128)(2,1)} %param.6) | copy-start | bytes 3145732
  6.5 140.4 %all-gather.3.cloned.1.call-start = ((), (), s32[]{:S(2)}) async-start(), calls=%async_computation.1 | async-start | bytes 13516800 | tf_op jit(solution)/shard_map/all_gather | solution.py:14
  25.4 219.1 %all-gather.5.cloned.1.call-start = ((), (), s32[]{:S(2)}) async-start(), calls=%async_computation.2 | async-start | bytes 8650752 | tf_op jit(solution)/shard_map/all_gather | solution.py:91
Sparse Core Ops, SparseCore 0:
  25.5 121.3 all-gather.2
  149.5 94.9 all-gather.4
where the time goes:
time: 258 us
  waiting for transfers between devices  184 us (71%)
  blocking collectives  26.8 us (10%)
  matrix products  26.3 us (10%)
  between operations  13.5 us (5%)
  other arithmetic  4.28 us (2%)
  local copies, waits for them, and re-layouts  2.62 us (1%)
    all_gather x1, waiting for transfers between devices, sent_together(): lax.all_gather(both, axis, axis=dim, tiled=True)  110 us
    all_gather x1, waiting for transfers between devices, body(): lax.all_gather(grouped_cols, 'fsdp', axis=1, tiled=True)  74.1 us
    all_gather x1, blocking collectives, sent_together(): lax.all_gather(both, axis, axis=dim, tiled=True)  17.1 us
    dot_general x1, matrix products, body(): queries = jnp.dot(normed, query_piece, preferred_element_type=jnp.float32)  10.6 us
    all_to_all x1, blocking collectives, copy_for_each(): return lax.all_to_all(copies, axis, split_axis=0, concat_axis=0, tiled=True)  9.7 us
    dot_general x1, matrix products, body(): jnp.dot(context, lax.all_gather(grouped_cols, 'fsdp', axis=1, tiled=True)...  6.74 us
  transfers between devices with their start and end apart: 2, of which 2 were waited for; matrix products, arithmetic and copies ran while one was open for 10% of the time, Pallas kernels for 0%

commit v1 on v0

--- a/solution.py
+++ b/solution.py
@@ -88,7 +88,9 @@
     grouped_cols = gather_directly(w_out, "rep", 1)
     branch = jnp.dot(
         context,
-        lax.all_gather(grouped_cols, "fsdp", axis=1, tiled=True),
+        jnp.concatenate(
+            lax.all_to_all(jnp.stack([grouped_cols] * lax.axis_size("fsdp")), "fsdp", 0, 0), axis=1
+        ),
         preferred_element_type=jnp.float32,
     )
     return (x_float + branch).astype(jnp.bfloat16)

time: 258 us -> 340 us (1.32); the launches traced: 258 us -> 335 us
  waiting for transfers between devices: 184 us -> 247 us
  starting transfers between devices: 0.04 us -> 11.1 us
  local copies, waits for them, and re-layouts: 2.62 us -> 6.85 us
    all_gather x1, waiting for transfers between devices: 110 us -> 247 us  [sent_together(): lax.all_gather(both, axis, axis=dim, tiled=True)]
    all_gather x1 -> x0, waiting for transfers between devices: 74.1 us -> none  [body(): lax.all_gather(grouped_cols, 'fsdp', axis=1, tiled=True)]
    all_to_all x0 -> x1, starting transfers between devices: none -> 11.1 us  [body(): lax.all_to_all(jnp.stack([grouped_cols] * lax.axis_size('fsdp')), 'fsdp',...]
    another operation x0 -> x1, local copies, waits for them, and re-layouts: none -> 4.32 us  [body(): jnp.stack([grouped_cols] * lax.axis_size('fsdp'))]
  transfers between devices with their start and end apart: 2 -> 2, of which waited for: 2 -> 1; matrix products, arithmetic and copies ran while one was open for 10% -> 9% of each run, Pallas kernels for 0% -> 0%
where the time goes in v1:
time: 340 us; the launch traced here: 335 us
  waiting for transfers between devices  247 us (73%)
  blocking collectives  26.3 us (8%)
  matrix products  26.3 us (8%)
  between operations  13.5 us (4%)
  starting transfers between devices  11.1 us (3%)
  local copies, waits for them, and re-layouts  6.85 us (2%)
  other arithmetic  4.28 us (1%)
    all_gather x1, waiting for transfers between devices, sent_together(): lax.all_gather(both, axis, axis=dim, tiled=True)  247 us
    all_gather x1, blocking collectives, sent_together(): lax.all_gather(both, axis, axis=dim, tiled=True)  17.1 us
    all_to_all x1, starting transfers between devices, body(): lax.all_to_all(jnp.stack([grouped_cols] * lax.axis_size('fsdp')), 'fsdp',...  11.1 us
    dot_general x1, matrix products, body(): queries = jnp.dot(normed, query_piece, preferred_element_type=jnp.float32)  10.6 us
    all_to_all x1, blocking collectives, copy_for_each(): return lax.all_to_all(copies, axis, split_axis=0, concat_axis=0, tiled=True)  9.16 us
  transfers between devices with their start and end apart: 2, of which 1 were waited for; matrix products, arithmetic and copies ran while one was open for 9% of the time, Pallas kernels for 0%

profile of v1, /device:TPU:1, one launch (start us, length us, event | category | flops | bytes accessed | tf_op | source)
XLA Modules:
  0.0 335.4 jit_solution(2032995712337194645)
XLA Ops:
  6.5 0.0 all-gather.2.cloned.1.call-start
  6.5 0.7 copy.17
  7.3 0.9 concatenate.17
  8.2 17.1 %all_gather.6 = bf16[64,3073]{1,0:T(8,128)(2,1)} all-gather(bf16[8,3073]{1,0:T(8,128)(2,1)S(1)} %concatenate.17), channel_id=1, replica_groups=mesh['fsdp'=32,'rep'=8] {'rep'}, dimensions={0}, use_global_device_ids=true | all-gather | bytes 442512 | tf_op jit(solution)/shard_map/all_gather | solution.py:14
  25.3 0.0 all-gather.2.cloned.1.call-update
  25.3 0.8 broadcast_in_dim.12
  26.1 9.2 %all_to_all.10 = bf16[8,2048,8]{1,2,0:T(8,128)(2,1)S(1)} all-to-all(bf16[8,2048,8]{1,2,0:T(8,128)(2,1)S(1)} %broadcast_in_dim.12), channel_id=1, replica_groups=mesh['fsdp'=32,'rep'=8] {'rep'}, dimensions={0} | all-to-all | bytes 524288 | tf_op jit(solution)/shard_map/all_to_all | solution.py:24
  35.2 4.3 %stack.3 = bf16[32,2048,64]{1,2,0:T(8,128)(2,1)} broadcast(bf16[2048,64]{0,1:T(8,128)(2,1)S(1)} %bitcast.40), dimensions={1,2} | broadcast | bytes 8650752 | tf_op jit(solution)/shard_map/stack | solution.py:92
  39.6 0.0 copy-start
  39.6 11.1 %all-to-all-start.1 = ((bf16[32,2048,64]{1,2,0:T(8,128)(2,1)}), bf16[32,2048,64]{1,2,0:T(8,128)(2,1)}, u32[]{:S(2)}, u32[]{:S(2)}) async-start(bf16[32,2048,64]{1,2,0:T(8,128)(2,1)} %stack.3), calls=%async_computation.1 | async-start | bytes 16777216 | tf_op jit(solution)/shard_map/all_to_all | solution.py:92
  50.7 0.2 fusion.33
  50.9 0.0 copy-done
  50.9 0.3 fusion.9
  51.2 247.1 %all-gather.2.cloned.1.call-done = bf16[2048,3073]{1,0:T(8,128)(2,1)} async-done(((bf16[64,3073]{1,0:T(8,128)(2,1)}), bf16[2048,3073]{1,0:T(8,128)(2,1)}) %all-gather.2.cloned.1.call-update) | async-done | bytes 12587024 | tf_op jit(solution)/shard_map/all_gather | solution.py:14
  298.3 1.3 convert_reduce_fusion
  299.6 2.9 fusion.19
  302.5 0.1 copy.18
  302.6 3.7 %fusion.12 = f32[256,512]{0,1:T(8,128)S(1)} fusion(bf16[2048,3073]{1,0:T(8,128)(2,1)} %all-gather.2.cloned.1.call-done, bf16[256,2048]{1,0:T(8,128)(2,1)S(1)} %copy-done, f32[2048]{0:T(1024)S(1)} %convert_reduce_fusion, f32[256]{0:T(256)S(1)} %add_rsqrt_fusion), kind=kOutput, calls=%fused_computation.18 | convolution fusion | flops 538968064 | bytes 3679232 | tf_op jit(solution)/shard_map/dot_general | solution.py:68
  306.4 10.6 %fusion.1 = f32[256,2048]{0,1:T(8,128)S(1)} fusion(bf16[2048,3073]{1,0:T(8,128)(2,1)} %all-gather.2.cloned.1.call-done, bf16[256,2048]{1,0:T(8,128)(2,1)S(1)} %copy-done, f32[2048]{0:T(1024)S(1)} %convert_reduce_fusion, f32[256]{0:T(256)S(1)} %add_rsqrt_fusion), kind=kOutput, calls=%fused_computation.1 | convolution fusion | flops 2149580800 | bytes 11543552 | tf_op jit(solution)/shard_map/dot_general | solution.py:67
  317.0 0.2 slice_negate_fusion
  317.1 1.5 fusion.22
  318.6 2.3 fusion.40
  320.9 0.9 fusion.18
  321.8 0.0 all-to-all-done.1
  321.8 6.7 %fusion.8 = bf16[256,2048]{1,0:T(8,128)(2,1)} fusion(bf16[256,2048]{0,1:T(8,128)(2,1)S(1)} %bitcast.43, bf16[2048,2048]{0,1:T(8,128)(2,1)} %bitcast.14, bf16[256,2048]{1,0:T(8,128)(2,1)S(1)} %copy-done), kind=kOutput, calls=%fused_computation.14 | convolution fusion | flops 2149056512 | bytes 11534336 | tf_op jit(solution)/shard_map/dot_general | solution.py:89
  (5 shorter events, 0.1 us)
Async XLA Ops:
  6.5 291.8 %all-gather.2.cloned.1.call-start = ((), (), s32[]{:S(2)}) async-start(), calls=%async_computation.2 | async-start | bytes 13516800 | tf_op jit(solution)/shard_map/all_gather | solution.py:14
  39.6 11.3 %copy-start = (bf16[256,2048]{1,0:T(8,128)(2,1)S(1)}, bf16[256,2048]{1,0:T(8,128)(2,1)}, u32[]{:S(2)}) copy-start(bf16[256,2048]{1,0:T(8,128)(2,1)} %param.6) | copy-start | bytes 3145732
  39.6 282.3 %all-to-all-start.1 = ((bf16[32,2048,64]{1,2,0:T(8,128)(2,1)}), bf16[32,2048,64]{1,2,0:T(8,128)(2,1)}, u32[]{:S(2)}, u32[]{:S(2)}) async-start(bf16[32,2048,64]{1,2,0:T(8,128)(2,1)} %stack.3), calls=%async_computation.1 | async-start | bytes 16777216 | tf_op jit(solution)/shard_map/all_to_all | solution.py:92
Sparse Core Ops, SparseCore 0:
  25.4 272.8 all-gather.1
